TPU v7x, 32 devices: a 4x2x2 block of a 4x4x8 slice. The times are simulated.
32 devices in a mesh: dp: 4 (over y, z), ep: 8 (over x, core).
Axes of the slice: x: 4, y: 2, z: 2, core: 2. Of those that a mesh axis runs over, the one named last changes fastest.
The devices are a block of a 4x4x8 slice.
Arguments:
- h0: bfloat16 [32, 256, 2048], P(('dp', 'ep')), parts along dimension 0
- idx: int32 [32, 256, 8], P(('dp', 'ep')), parts along dimension 0
- slot: int32 [32, 256, 8], P(('dp', 'ep')), parts along dimension 0
- norm_attn: bfloat16 [2048], replicated
- wq: bfloat16 [2048, 2048], replicated
- wk: bfloat16 [2048, 2048], replicated
- wv: bfloat16 [2048, 2048], replicated
- wo: bfloat16 [2048, 2048], replicated
- norm_ffn: bfloat16 [2048], replicated
- w1: bfloat16 [2048, 8192], replicated
- w3: bfloat16 [2048, 8192], replicated
- w2: bfloat16 [8192, 2048], replicated
- norm_moe: bfloat16 [2048], replicated
- wr: bfloat16 [2048, 64], replicated
- ue1: bfloat16 [64, 2048, 1024], P('ep')
- ue3: bfloat16 [64, 2048, 1024], P('ep')
- ue2: bfloat16 [64, 1024, 2048], P('ep')
Outputs:
- output: bfloat16 [32, 256, 2048], P(('dp', 'ep')), parts along dimension 0
There are 4 independent parts. A program takes and returns all parts, laid end to end along the dimension named above; an argument that names none is the same for every part.
All inputs are finite; a program needn't handle non-finite values.
Results may differ from a plain program's by a relative error of at most 0.0105726.
Values are sent between devices in bfloat16 or wider.
A program may use at most 768 MiB of HBM per device.

v0:
```python
import jax
import jax.numpy as jnp
from jax import lax
from jax.sharding import PartitionSpec as P

HEAD = 128
EPS = 1e-6
ROPE_BASE = 10000.0


def _rms(x, w):
    xf = x.astype(jnp.float32)
    r = lax.rsqrt(jnp.mean(xf * xf, axis=-1, keepdims=True) + EPS)
    return (xf * r * w.astype(jnp.float32)).astype(jnp.bfloat16)


def _rope(x, cos, sin):
    h = HEAD // 2
    x1, x2 = x[..., :h], x[..., h:]
    return jnp.concatenate([x1 * cos - x2 * sin, x2 * cos + x1 * sin], axis=-1)


def _dense(h0, na, wq, wk, wv, wo, nf, w1, w3, w2):
    f32, bf = jnp.float32, jnp.bfloat16
    b, s, d = h0.shape
    nh = wq.shape[1] // HEAD
    nkvv = wk.shape[1] // HEAD
    pos = jnp.arange(s).astype(f32)
    inv = ROPE_BASE ** (-2.0 * jnp.arange(HEAD // 2).astype(f32) / HEAD)
    ang = pos[:, None] * inv[None, :]
    cos, sin = jnp.cos(ang)[:, None, :], jnp.sin(ang)[:, None, :]
    x = _rms(h0, na).reshape(b * s, d)
    q = _rope(jnp.dot(x, wq, preferred_element_type=f32).reshape(b, s, nh, HEAD), cos, sin).astype(bf)
    k = _rope(jnp.dot(x, wk, preferred_element_type=f32).reshape(b, s, nkvv, HEAD), cos, sin).astype(bf)
    v = jnp.dot(x, wv, preferred_element_type=f32).astype(bf).reshape(b, s, nkvv, HEAD)
    q = q.reshape(b, s, nkvv, nh // nkvv, HEAD)
    sc = jnp.einsum('bqgrd,bkgd->bgrqk', q, k, preferred_element_type=f32) * HEAD ** -0.5
    causal = jnp.arange(s)[:, None] >= jnp.arange(s)[None, :]
    sc = jnp.where(causal, sc, -jnp.inf)
    p = jax.nn.softmax(sc, axis=-1).astype(bf)
    o = jnp.einsum('bgrqk,bkgd->bqgrd', p, v, preferred_element_type=f32).astype(bf).reshape(b * s, nh * HEAD)
    a = (h0.reshape(b * s, d).astype(f32) + jnp.dot(o, wo, preferred_element_type=f32)).astype(bf)
    z = _rms(a, nf)
    hid = (jax.nn.silu(jnp.dot(z, w1, preferred_element_type=f32)) * jnp.dot(z, w3, preferred_element_type=f32)).astype(bf)
    return a.astype(f32) + jnp.dot(hid, w2, preferred_element_type=f32)


def _route(h0, nm, wr, idx):
    d = h0.shape[-1]
    k = idx.shape[-1]
    u = _rms(h0, nm).reshape(-1, d)
    logits = jnp.dot(u, wr, preferred_element_type=jnp.float32)
    g = jax.nn.softmax(jnp.take_along_axis(logits, idx.reshape(-1, k), axis=1), axis=-1)
    return u, g


def _experts(x, ue1, ue3, ue2):
    f32 = jnp.float32
    h1 = jnp.einsum('ecd,edf->ecf', x, ue1, preferred_element_type=f32)
    h3 = jnp.einsum('ecd,edf->ecf', x, ue3, preferred_element_type=f32)
    hid = (jax.nn.silu(h1) * h3).astype(jnp.bfloat16)
    return jnp.einsum('ecf,efd->ecd', hid, ue2, preferred_element_type=f32).astype(jnp.bfloat16)


def solution(mesh):
    G = mesh.shape['ep']

    def local(h0, idx, slot, na, wq, wk, wv, wo, nf, w1, w3, w2, nm, wr, ue1, ue3, ue2):
        f32 = jnp.float32
        b, s, d = h0.shape
        t = b * s
        k = idx.shape[-1]
        el = ue1.shape[0]
        e = el * G
        cap = 2 * t * k // e
        u, g = _route(h0, nm, wr, idx)
        ix = idx.reshape(t, k)
        sl = slot.reshape(t, k)
        rows = jnp.broadcast_to(jnp.arange(t, dtype=jnp.int32)[:, None], (t, k))
        tok = jnp.full((e, cap), t, jnp.int32).at[ix, sl].set(rows)
        send = jnp.take(u, tok, axis=0, mode='fill', fill_value=0)
        recv = lax.all_to_all(send, 'ep', 0, 0, tiled=True)
        x = recv.reshape(G, el, cap, d).transpose(1, 0, 2, 3).reshape(el, G * cap, d)
        y = _experts(x, ue1, ue3, ue2)
        y = y.reshape(el, G, cap, d).transpose(1, 0, 2, 3).reshape(e, cap, d)
        back = lax.all_to_all(y, 'ep', 0, 0, tiled=True)
        yg = back[ix, sl]
        m = jnp.sum(g[..., None] * yg.astype(f32), axis=1)
        dense = _dense(h0, na, wq, wk, wv, wo, nf, w1, w3, w2)
        return (dense + m).astype(jnp.bfloat16).reshape(b, s, d)

    rows_spec = P(('dp', 'ep'))
    in_specs = (rows_spec,) * 3 + (P(),) * 11 + (P('ep'),) * 3
    return jax.shard_map(local, mesh=mesh, in_specs=in_specs, out_specs=rows_spec, check_vma=False)
```

profile of v0, /device:TPU:81, one launch (start us, length us, event | category | flops | bytes accessed | tf_op | source)
XLA Modules:
  0.0 612.7 jit_solution(15601466451441794047)
XLA Ops:
  0.0 1.4 shift-left_or_fusion
  1.4 0.7 multiply_reduce_fusion
  2.5 8.1 %scatter_custom_fusion = s32[4096]{0:T(1024)S(1)} fusion(s32[2048]{0:T(1024)S(1)} %reshape.352, s32[2048]{0:T(1024)S(1)} %reshape.354, s32[]{:T(128)} %constant.59.clone.1), kind=kCustom, calls=%fused_computation.89 | custom fusion | bytes 16388
  10.7 0.7 convert_element_type.133
  11.3 1.5 fusion.20
  13.0 1.5 fusion.31
  14.5 21.0 %gather_fusion = bf16[4096,2048]{1,0:T(8,128)(2,1)} fusion(bf16[256,2048]{1,0:T(8,128)(2,1)S(1)} %fusion.31, s32[4096]{0:T(1024)S(1)} %broadcast_clamp_fusion), kind=kCustom, calls=%fused_computation | custom fusion | bytes 33570816 | tf_op jit(solution)/shard_map/jit(_take)/gather | solution.py:81
  35.5 8.3 %broadcast_select_fusion = bf16[64,64,2048]{2,1,0:T(8,128)(2,1)S(1)} fusion(bf16[64,64,2048]{2,1,0:T(8,128)(2,1)} %bitcast.115, pred[64,64]{1,0:T(8,128)(4,1)S(1)} %compare_and_fusion), kind=kLoop, calls=%fused_computation.7 | loop fusion | flops 8388608 | bytes 33558528 | tf_op jit(solution)/shard_map/jit(_take)/select_n | solution.py:81
  43.8 189.3 %all_to_all.10 = bf16[64,64,2048]{2,1,0:T(8,128)(2,1)S(1)} all-to-all(bf16[64,64,2048]{2,1,0:T(8,128)(2,1)S(1)} %broadcast_select_fusion), channel_id=1, replica_groups=mesh['dp'=4,'ep'=8] {'ep'}, dimensions={0} | all-to-all | bytes 33554432 | tf_op jit(solution)/shard_map/all_to_all | solution.py:82
  233.1 6.6 %copy.46 = bf16[8,8,64,2048]{3,2,1,0:T(8,128)(2,1)} copy(bf16[8,8,64,2048]{3,2,0,1:T(8,128)(2,1)S(1)} %bitcast.117) | data formatting | bytes 33554432 | tf_op jit(solution)/shard_map/transpose | solution.py:83
  239.7 31.9 %fusion.66 = f32[8,512,1024]{2,1,0:T(8,128)} fusion(bf16[8,512,2048]{2,1,0:T(8,128)(2,1)} %bitcast.120, bf16[8,2048,1024]{2,1,0:T(8,128)(2,1)} %param.31), kind=kOutput, calls=%fused_computation.103 | convolution fusion | flops 17179869184 | bytes 67108864 | tf_op jit(solution)/shard_map/ecd,edf->ecf/dot_general | solution.py:59
  271.6 45.4 %convolution_convert_fusion = bf16[8,512,2048]{2,1,0:T(8,128)(2,1)} fusion(bf16[8,1024,2048]{2,1,0:T(8,128)(2,1)} %param.33, f32[8,512,1024]{2,1,0:T(8,128)} %fusion.66, bf16[8,512,2048]{2,1,0:T(8,128)(2,1)} %bitcast.121, bf16[8,2048,1024]{2,1,0:T(8,128)(2,1)} %param.32), kind=kOutput, calls=%fused_computation.8 | convolution fusion | flops 34393292800 | bytes 117440512 | tf_op jit(solution)/shard_map/ecf,efd->ecd/dot_general | solution.py:62
  316.9 14.1 %copy.47 = bf16[8,8,64,2048]{3,2,1,0:T(8,128)(2,1)} copy(bf16[8,8,64,2048]{3,2,0,1:T(8,128)(2,1)} %bitcast.122) | data formatting | bytes 33554432 | tf_op jit(solution)/shard_map/transpose | solution.py:85
  331.0 7.1 %all-to-all-start.1 = ((bf16[64,64,2048]{2,1,0:T(8,128)(2,1)}), bf16[64,64,2048]{2,1,0:T(8,128)(2,1)}, u32[]{:S(2)}, u32[]{:S(2)}) async-start(bf16[64,64,2048]{2,1,0:T(8,128)(2,1)} %bitcast.116), calls=%async_computation.1 | async-start | bytes 33554432 | tf_op jit(solution)/shard_map/all_to_all | solution.py:86
  339.3 16.8 %gather_fusion.2 = f32[2048]{0:T(1024)S(1)} fusion(f32[256,64]{0,1:T(8,128)S(1)} %fusion.65, s32[2048]{0:T(1024)S(1)} %reshape.346), kind=kCustom, calls=%fused_computation.2 | custom fusion | bytes 32768 | tf_op jit(solution)/shard_map/jit(take_along_axis)/gather | solution.py:53
  356.3 6.8 %convolution_convert_fusion.1 = bf16[256,2048]{1,0:T(8,128)(2,1)} fusion(bf16[2048,2048]{1,0:T(8,128)(2,1)} %param.23, bf16[1,256,2048]{2,1,0:T(8,128)(2,1)S(1)} %copy-done.4, f32[2048]{0:T(1024)S(1)} %convert_element_type.119, f32[256]{0:T(256)S(1)} %copy-done.9), kind=kOutput, calls=%fused_computation.31 | convolution fusion | flops 2150105088 | bytes 10494976 | tf_op jit(solution)/shard_map/dot_general | solution.py:35
  363.0 1.5 copy.52
  364.5 12.3 %copy.54 = bf16[2048,2048]{1,0:T(8,128)(2,1)} copy(bf16[2048,2048]{0,1:T(8,128)(2,1)} %bitcast.123) | data formatting | bytes 16777216 | tf_op jit(solution)/shard_map/dot_general | solution.py:33
  376.8 12.3 %copy.53 = bf16[2048,2048]{1,0:T(8,128)(2,1)} copy(bf16[2048,2048]{0,1:T(8,128)(2,1)} %bitcast.124) | data formatting | bytes 16777216 | tf_op jit(solution)/shard_map/dot_general | solution.py:34
  389.8 6.1 convolution_bitcast_fusion
  396.0 2.5 convolution_bitcast_fusion.1
  398.5 0.7 fusion.50
  399.1 0.9 fusion.8
  400.1 0.9 fusion.7
  401.0 1.3 fusion.24
  402.3 1.5 slice-done.1
  403.8 2.5 fusion.17
  406.4 17.3 %fusion.29 = f32[256,8192]{1,0:T(8,128)} fusion(bf16[2048,8192]{1,0:T(8,128)(2,1)} %param.26, bf16[256,2048]{1,0:T(8,128)(2,1)S(1)} %get-tuple-element.20, f32[2048]{0:T(1024)S(1)} %convert_element_type.130, f32[256]{0:T(256)S(1)} %add_rsqrt_fusion), kind=kOutput, calls=%fused_computation.47 | convolution fusion | flops 8592031744 | bytes 43000832 | tf_op jit(solution)/shard_map/dot_general | solution.py:44
  423.8 97.8 %all-to-all-done.1 = bf16[64,64,2048]{2,1,0:T(8,128)(2,1)} async-done(((bf16[64,64,2048]{2,1,0:T(8,128)(2,1)}), bf16[64,64,2048]{2,1,0:T(8,128)(2,1)}, u32[]{:S(2)}, u32[]{:S(2)}) %all-to-all-start.1) | async-done | bytes 16777248 | tf_op jit(solution)/shard_map/all_to_all | solution.py:86
  521.6 50.4 %gather_fusion.1 = bf16[2048,2048]{1,0:T(8,128)(2,1)} fusion(bf16[64,64,2048]{2,1,0:T(8,128)(2,1)} %all-to-all-done.1, s32[2048]{0:T(1024)S(1)} %reshape.340), kind=kCustom, calls=%fused_computation.1 | custom fusion | bytes 16793600 | tf_op jit(solution)/shard_map/gather | solution.py:87
  572.0 11.2 %fusion = f32[256,2048]{1,0:T(8,128)S(1)} fusion(bf16[2048,2048]{1,0:T(8,128)(2,1)} %gather_fusion.1, f32[256,8]{1,0:T(8,128)S(1)} %fusion.52), kind=kLoop, calls=%fused_computation.5 | loop fusion | flops 12058624 | bytes 10493952 | tf_op jit(solution)/shard_map/reduce_sum | solution.py:88
  583.2 29.1 %fusion.14 = bf16[1,256,2048]{2,1,0:T(8,128)(2,1)} fusion(f32[256,2048]{1,0:T(8,128)S(1)} %fusion, bf16[8192,2048]{1,0:T(8,128)(2,1)} %param.28, bf16[2048,8192]{1,0:T(8,128)(2,1)} %param.27, f32[256,8192]{1,0:T(8,128)} %fusion.29, bf16[256,2048]{1,0:T(8,128)(2,1)S(1)} %get-tuple-element.20, f32[2048]{0:T(1024)S(1)} %convert_element_type.130, ...), kind=kOutput, calls=%fused_computation.34 | convolution fusion | flops 17196646400 | bytes 79700992 | tf_op jit(solution)/shard_map/dot_general | solution.py:45
  (62 shorter events, 2.6 us)
Async XLA Ops:
  0.0 338.8 %copy-start = (bf16[2048,64]{0,1:T(8,128)(2,1)S(1)}, bf16[2048,64]{0,1:T(8,128)(2,1)}, u32[]{:S(2)}) copy-start(bf16[2048,64]{0,1:T(8,128)(2,1)} %param.30) | copy-start | bytes 786436
  12.9 22.6 %copy-start.8 = (f32[256]{0:T(256)}, f32[256]{0:T(256)S(1)}, u32[]{:S(2)}) copy-start(f32[256]{0:T(256)S(1)} %add_rsqrt_fusion.1) | copy-start | bytes 3076
  14.5 21.0 %copy-start.2 = (bf16[256,2048]{1,0:T(8,128)(2,1)}, bf16[256,2048]{1,0:T(8,128)(2,1)S(1)}, u32[]{:S(2)}) copy-start(bf16[256,2048]{1,0:T(8,128)(2,1)S(1)} %fusion.31) | copy-start | bytes 3145732
  331.0 7.2 %copy-start.5 = (s32[1,256,8]{1,2,0:T(8,128)S(1)}, s32[1,256,8]{1,2,0:T(8,128)}, u32[]{:S(2)}) copy-start(s32[1,256,8]{1,2,0:T(8,128)} %param.18) | copy-start | bytes 24580
  331.0 7.3 %copy-start.7 = (s32[256,8,1]{0,1,2:T(8,128)S(1)}, s32[256,8,1]{0,1,2:T(8,128)}, u32[]{:S(2)}) copy-start(s32[256,8,1]{0,1,2:T(8,128)} %get-tuple-element.12) | copy-start | bytes 24580
  331.0 7.6 %copy-start.6 = (s32[256,8,1]{0,1,2:T(8,128)S(1)}, s32[256,8,1]{0,1,2:T(8,128)}, u32[]{:S(2)}) copy-start(s32[256,8,1]{0,1,2:T(8,128)} %get-tuple-element.11) | copy-start | bytes 24580
  331.0 7.8 %copy-start.3 = (bf16[256,2048]{1,0:T(8,128)(2,1)S(1)}, bf16[256,2048]{1,0:T(8,128)(2,1)}, u32[]{:S(2)}) copy-start(bf16[256,2048]{1,0:T(8,128)(2,1)} %copy-done.2) | copy-start | bytes 3145732
  331.0 190.5 %all-to-all-start.1 = ((bf16[64,64,2048]{2,1,0:T(8,128)(2,1)}), bf16[64,64,2048]{2,1,0:T(8,128)(2,1)}, u32[]{:S(2)}, u32[]{:S(2)}) async-start(bf16[64,64,2048]{2,1,0:T(8,128)(2,1)} %bitcast.116), calls=%async_computation.1 | async-start | bytes 33554432 | tf_op jit(solution)/shard_map/all_to_all | solution.py:86
  339.3 16.9 %copy-start.10 = (bf16[2048]{0:T(1024)(128)(2,1)S(1)}, bf16[2048]{0:T(1024)(128)(2,1)}, u32[]{:S(2)}) copy-start(bf16[2048]{0:T(1024)(128)(2,1)} %param.20) | copy-start | bytes 12292
  339.3 16.9 %copy-start.4 = (bf16[1,256,2048]{2,1,0:T(8,128)(2,1)S(1)}, bf16[1,256,2048]{2,1,0:T(8,128)(2,1)}, u32[]{:S(2)}) copy-start(bf16[1,256,2048]{2,1,0:T(8,128)(2,1)} %param.17) | copy-start | bytes 3145732
  339.3 16.9 %copy-start.9 = (f32[256]{0:T(256)S(1)}, f32[256]{0:T(256)}, u32[]{:S(2)}) copy-start(f32[256]{0:T(256)} %copy-done.8) | copy-start | bytes 3076
  376.8 12.3 %copy-start.11 = (bf16[2048]{0:T(1024)(128)(2,1)S(1)}, bf16[2048]{0:T(1024)(128)(2,1)}, u32[]{:S(2)}) copy-start(bf16[2048]{0:T(1024)(128)(2,1)} %param.25) | copy-start | bytes 12292
  389.3 6.6 %slice-start.2 = ((s8[8388608]{0:T(1024)(128)(4,1)}), s8[4194304]{0:T(1024)(128)(4,1)S(1)}, s32[]{:S(2)}) async-start(s8[8388608]{0:T(1024)(128)(4,1)} %bitcast.125), calls=%async_computation.4 | async-start | bytes 8388608
  389.8 6.1 %slice-start.3 = ((s8[8388608]{0:T(1024)(128)(4,1)}), s8[4194304]{0:T(1024)(128)(4,1)S(1)}, s32[]{:S(2)}) async-start(s8[8388608]{0:T(1024)(128)(4,1)} %bitcast.125), calls=%async_computation.5 | async-start | bytes 8388608
  400.1 2.2 slice-start
  401.0 2.8 slice-start.1
  583.2 29.2 %copy-start.1 = (bf16[2048,64]{0,1:T(8,128)(2,1)S(1)}, bf16[2048,64]{0,1:T(8,128)(2,1)}, u32[]{:S(2)}) copy-start(bf16[2048,64]{0,1:T(8,128)(2,1)} %param.30) | copy-start | bytes 786436
where the time goes:
time: 623 us; the launch traced here: 613 us
  blocking collectives  189 us (30%)
  local copies, waits for them, and re-layouts  146 us (23%)
  matrix products  144 us (23%)
  waiting for transfers between devices  97.8 us (16%)
  other arithmetic  27.7 us (4%)
  starting transfers between devices  7.15 us (1%)
    all_to_all x1, blocking collectives, local(): recv = lax.all_to_all(send, 'ep', 0, 0, tiled=True)  189 us
    all_to_all x1, waiting for transfers between devices, local(): back = lax.all_to_all(y, 'ep', 0, 0, tiled=True)  97.8 us
    gather x1, local copies, waits for them, and re-layouts, local(): yg = back[ix, sl]  50.4 us
    dot_general x1, matrix products, _experts(): jnp.einsum('ecf,efd->ecd', hid, ue2, preferred_element_type=f32)  45.4 us
    dot_general x1, matrix products, _experts(): h1 = jnp.einsum('ecd,edf->ecf', x, ue1, preferred_element_type=f32)  31.9 us
    dot_general x1, matrix products, _dense(): return a.astype(f32) + jnp.dot(hid, w2, preferred_element_type=f32)  29.1 us
    gather x1, local copies, waits for them, and re-layouts, local(): send = jnp.take(u, tok, axis=0, mode='fill', fill_value=0)  21 us
    dot_general x1, matrix products, _dense(): jnp.dot(z, w1, preferred_element_type=f32)  17.3 us
  transfers between devices with their start and end apart: 1, of which 1 were waited for; matrix products, arithmetic and copies ran while one was open for 14% of the time, Pallas kernels for 0%

commit v1 on v0

v1 whole, which is shorter than its diff:
```python
import functools

import jax
import jax.numpy as jnp
from jax import lax
from jax.experimental import pallas as pl
from jax.experimental.pallas import tpu as pltpu
from jax.sharding import PartitionSpec as P

HEAD = 128
EPS = 1e-6
ROPE_BASE = 10000.0
MiB = 1 << 20
f32, bf16 = jnp.float32, jnp.bfloat16
MESH = pl.DeviceIdType.MESH


def _dot(a, b):
    return jnp.dot(a, b, preferred_element_type=f32)


def _norm(x, w):
    xf = x.astype(f32)
    r = lax.rsqrt(jnp.mean(xf * xf, axis=-1, keepdims=True) + EPS)
    return (xf * r * w.astype(f32)).astype(bf16)


def _loop(n, body):
    lax.fori_loop(0, n, lambda i, c: (body(i), c)[1], 0)


def _place(chips):
    me = lax.axis_index('ep')
    x, c = me // 2, me % 2
    return me, lambda dx, fc: lax.rem(x + dx, chips) * 2 + (lax.rem(c + fc, 2))


def _remote(src, dst, ssem, rsem, dev):
    return pltpu.make_async_remote_copy(src_ref=src, dst_ref=dst, send_sem=ssem, recv_sem=rsem,
                                        device_id={'ep': dev}, device_id_type=MESH)


def _greet(devs):
    bar = pltpu.get_barrier_semaphore()
    for d in devs:
        pl.semaphore_signal(bar, inc=1, device_id={'ep': d}, device_id_type=MESH)
    pl.semaphore_wait(bar, len(devs))


def _front_kernel(chips, k, cap, fb, hb,
                  h_ref, nm_ref, wrt_ref, idx_ref, slot_ref, na_ref, nf_ref, cos_ref, sin_ref,
                  wq_ref, wk_ref, wv_ref, wo_ref, ue1_ref, ue3_ref,
                  hid_ref, c_ref, a_ref, z_ref,
                  uall, maps, mall, xg, xa, acc, aring, bring, ering, hstage, cstage,
                  asem, esem, hsem, csem, usend, urecv, msend, mrecv):
    n = 2 * chips
    me, dev = _place(chips)
    t, d = h_ref.shape
    half = t // 2
    el = ue1_ref.shape[0]
    fe = ue1_ref.shape[2]
    wb = hb * HEAD
    ng = wq_ref.shape[1] // wb
    nf = fe // fb
    steps = el * nf
    deep = ering.shape[0]

    def attn_in(g, s):
        col = pl.ds(pl.multiple_of(g * wb, wb), wb)
        return [pltpu.make_async_copy(w.at[:, col], aring.at[s, i], asem.at[s, i])
                for i, w in enumerate((wq_ref, wk_ref, wv_ref))] + [
            pltpu.make_async_copy(wo_ref.at[col, :], bring.at[s], asem.at[s, 3])]

    def exp_in(i, s):
        e, j = i // nf, i % nf
        col = pl.ds(pl.multiple_of(j * fb, fb), fb)
        return [pltpu.make_async_copy(w.at[e, :, col], ering.at[s, q], esem.at[s, q])
                for q, w in enumerate((ue1_ref, ue3_ref))]

    for s in range(2):
        for cp in attn_in(s, s):
            cp.start()

    u = _norm(h_ref[...], nm_ref[...])
    uall[0] = u
    lt = lax.dot_general(wrt_ref[...], u, (((1,), (1,)), ((), ())), preferred_element_type=f32)
    ids = lax.broadcasted_iota(jnp.int32, lt.shape, 0)
    hits = [ids == idx_ref[j:j + 1, :] for j in range(k)]
    sel = [jnp.sum(jnp.where(h, lt, 0.0), axis=0, keepdims=True) for h in hits]
    top = functools.reduce(jnp.maximum, sel)
    ex = [jnp.exp(s - top) for s in sel]
    den = functools.reduce(jnp.add, ex)
    gate = jnp.zeros(lt.shape, f32)
    slot = jnp.full(lt.shape, -1.0, f32)
    for j in range(k):
        gate = jnp.where(hits[j], ex[j] / den, gate)
        slot = jnp.where(hits[j], slot_ref[j:j + 1, :].astype(f32), slot)
    maps[0] = slot
    maps[1] = gate
    xa[...] = _norm(h_ref[...], na_ref[...])
    acc[...] = jnp.zeros_like(acc)

    rel = [(p // 2, p % 2) for p in range(n)]
    others = [dev(*r) for r in rel[1:]]
    _greet(others)
    own = pl.ds(pl.multiple_of(me * el, el), el)
    mall[0] = maps[:, own, :]

    lo, hi = pl.ds(0, half), pl.ds(half, half)
    right, left, pair = dev(1, 0), dev(chips - 1, 0), dev(0, 1)
    hop = lambda i, a, b, rows, to: _remote(uall.at[a, rows], uall.at[b, rows], usend.at[i], urecv.at[i], to)
    r1, l1 = hop(0, 0, 2, lo, right), hop(1, 0, 6, hi, left)
    r2, l2 = hop(2, 0, 2, hi, right), hop(3, 0, 6, lo, left)
    p0 = hop(4, 0, 1, pl.ds(0, t), pair)
    ro, lo_ = hop(5, 2, 4, lo, right), hop(6, 6, 4, hi, left)
    p1, p3 = hop(7, 2, 3, pl.ds(0, t), pair), hop(8, 6, 7, pl.ds(0, t), pair)
    p2 = hop(9, 4, 5, pl.ds(0, t), pair)
    metas = [_remote(maps.at[:, pl.ds(pl.multiple_of(o * el, el), el), :], mall.at[p + 1],
                     msend.at[p], mrecv.at[p], o) for p, o in enumerate(others)]
    for m in metas:
        m.start()
    for m in (r1, l1, p0, r2, l2):
        m.start()
    for s in range(deep):
        for cp in exp_in(s, s):
            cp.start()

    def head_group(g):
        s = lax.rem(g, 2)
        for cp in attn_in(g, s):
            cp.wait()
        x = xa[...]
        q = _dot(x, aring[s, 0])
        kk = _dot(x, aring[s, 1])
        v = _dot(x, aring[s, 2]).astype(bf16)
        cos, sin = cos_ref[...], sin_ref[...]
        causal = lax.broadcasted_iota(jnp.int32, (t, t), 0) >= lax.broadcasted_iota(jnp.int32, (t, t), 1)
        outs = []
        for hd in range(hb):
            sl = slice(hd * HEAD, (hd + 1) * HEAD)
            qh = (q[:, sl] * cos + pltpu.roll(q[:, sl], HEAD // 2, 1) * sin).astype(bf16)
            kh = (kk[:, sl] * cos + pltpu.roll(kk[:, sl], HEAD // 2, 1) * sin).astype(bf16)
            sc = lax.dot_general(qh, kh, (((1,), (1,)), ((), ())), preferred_element_type=f32) * HEAD ** -0.5
            sc = jnp.where(causal, sc, -jnp.inf)
            e = jnp.exp(sc - jnp.max(sc, axis=-1, keepdims=True))
            pr = (e / jnp.sum(e, axis=-1, keepdims=True)).astype(bf16)
            outs.append(_dot(pr, v[:, sl]).astype(bf16))
        acc[...] += _dot(jnp.concatenate(outs, axis=1), bring[s])

        @pl.when(g + 2 < ng)
        def _():
            for cp in attn_in(g + 2, s):
                cp.start()

    _loop(ng, head_group)
    a = (h_ref[...].astype(f32) + acc[...]).astype(bf16)
    a_ref[...] = a
    z_ref[...] = _norm(a, nf_ref[...])

    r1.wait_recv()
    l1.wait_recv()
    ro.start()
    lo_.start()

    for m in metas:
        m.wait_recv()
    tm = jnp.concatenate([mall[p, 0] for p in range(n)] + [mall[p, 1] for p in range(n)], axis=0).T
    g1 = tm.astype(bf16)
    r = tm - g1.astype(f32)
    g2 = r.astype(bf16)
    g3 = (r - g2.astype(f32)).astype(bf16)
    lanes = lax.broadcasted_iota(jnp.int32, (t, el * cap), 1)
    lane_slot = lax.rem(lanes, cap).astype(f32)
    rows_i = lax.broadcasted_iota(jnp.int32, (tm.shape[1], el * cap), 0)
    cols_e = lax.broadcasted_iota(jnp.int32, (tm.shape[1], el * cap), 1) // cap

    def c_out(s, b):
        return pltpu.make_async_copy(cstage.at[b], c_ref.at[s], csem.at[b])

    def gates(s):
        b = lax.rem(s, 2)

        @pl.when(s >= 2)
        def _():
            c_out(s - 2, b).wait()

        pick_s = (rows_i == cols_e + s * el).astype(f32).astype(bf16)
        pick_g = (rows_i == cols_e + (s + n) * el).astype(f32).astype(bf16)
        hit = _dot(g1, pick_s) == lane_slot
        for i, g in enumerate((g1, g2, g3)):
            cstage[b, i * t:(i + 1) * t, :] = jnp.where(hit, _dot(g, pick_g), 0.0).astype(bf16)
        c_out(s, b).start()

    _loop(n, gates)
    for s in range(n - 2, n):
        c_out(s, s % 2).wait()

    slots_i = lax.broadcasted_iota(jnp.int32, (cap, t), 0).astype(f32)
    hs = n // 2
    rows = hs * cap

    def h_out(i, b, part):
        e, j = i // nf, i % nf
        return pltpu.make_async_copy(
            hstage.at[b], hid_ref.at[e, pl.ds(part * rows, rows), pl.ds(pl.multiple_of(j * fb, fb), fb)], hsem.at[b])

    def gather(part):
        def one(s):
            p = part * hs + s
            oh = jnp.concatenate([(slots_i == mall[p, 0, e:e + 1, :]).astype(f32).astype(bf16) for e in range(el)], axis=0)
            for c in range(0, d, 512):
                g = _dot(oh, uall[p, :, c:c + 512]).astype(bf16)
                for e in range(el):
                    xg[e, pl.ds(pl.multiple_of(s * cap, cap), cap), c:c + 512] = g[e * cap:(e + 1) * cap]
        _loop(hs, one)

    def hidden(part):
        def one(i):
            gi = part * steps + i
            s = lax.rem(gi, deep)
            b = lax.rem(i, 2)
            for cp in exp_in(i, s):
                cp.wait()
            x = xg[i // nf]
            h1 = _dot(x, ering[s, 0])
            h3 = _dot(x, ering[s, 1])

            @pl.when(i >= 2)
            def _():
                h_out(i - 2, b, part).wait()

            hstage[b] = (h1 * jax.nn.sigmoid(h1) * h3).astype(bf16)
            h_out(i, b, part).start()

            @pl.when(gi + deep < 2 * steps)
            def _():
                for cp in exp_in(lax.rem(i + deep, steps), s):
                    cp.start()

            if part == 0:
                @pl.when(i == (3 * steps) // 4)
                def _():
                    ro.wait_recv()
                    lo_.wait_recv()
                    p2.start()
        _loop(steps, one)
        for i in range(steps - 2, steps):
            h_out(i, i % 2, part).wait()

    r2.wait_recv()
    l2.wait_recv()
    p1.start()
    p3.start()
    p0.wait_recv()
    p1.wait_recv()
    gather(0)
    hidden(0)
    p3.wait_recv()
    p2.wait_recv()
    gather(1)
    hidden(1)
    for m in metas + [r1, l1, r2, l2, p0, ro, lo_, p1, p3, p2]:
        m.wait_send()


def _front(chips, cap, h, nm, wrt, idxt, slott, na, nf, cos, sin, wq, wk, wv, wo, ue1, ue3, fb=512, hb=4, deep=3):
    t, d = h.shape
    el, _, fe = ue1.shape
    n = 2 * chips
    k = idxt.shape[0]
    e = wrt.shape[0]
    vm, hbm = pl.BlockSpec(memory_space=pltpu.VMEM), pl.BlockSpec(memory_space=pl.ANY)
    dma = pltpu.SemaphoreType.DMA
    return pl.pallas_call(
        functools.partial(_front_kernel, chips, k, cap, fb, hb),
        in_specs=[vm] * 9 + [hbm] * 6,
        out_specs=[hbm, hbm, vm, vm],
        out_shape=(jax.ShapeDtypeStruct((el, n * cap, fe), bf16), jax.ShapeDtypeStruct((n, 3 * t, el * cap), bf16),
                   jax.ShapeDtypeStruct((t, d), bf16), jax.ShapeDtypeStruct((t, d), bf16)),
        scratch_shapes=[
            pltpu.VMEM((n, t, d), bf16), pltpu.VMEM((2, e, t), f32), pltpu.VMEM((n, 2, el, t), f32),
            pltpu.VMEM((el, n // 2 * cap, d), bf16), pltpu.VMEM((t, d), bf16), pltpu.VMEM((t, d), f32),
            pltpu.VMEM((2, 3, d, hb * HEAD), bf16), pltpu.VMEM((2, hb * HEAD, d), bf16),
            pltpu.VMEM((deep, 2, d, fb), bf16), pltpu.VMEM((2, n // 2 * cap, fb), bf16),
            pltpu.VMEM((2, 3 * t, el * cap), bf16),
            dma((2, 4)), dma((deep, 2)), dma((2,)), dma((2,)), dma((10,)), dma((10,)), dma((n - 1,)), dma((n - 1,)),
        ],
        compiler_params=pltpu.CompilerParams(vmem_limit_bytes=63 * MiB, collective_id=0, has_side_effects=True),
        name="front",
    )(h, nm, wrt, idxt, slott, na, nf, cos, sin, wq, wk, wv, wo, ue1, ue3)


def _back_kernel(chips, cap, cb, fb, z_ref, a_ref, hid_ref, c_hbm, ue2_ref, w1_ref, w3_ref, w2_ref, out_ref,
                 cbuf, hring, ering, y, p, got, part, relay, home, acc, fup, fdn,
                 csem, osem, fsem, dsend, drecv, rsend, rrecv):
    n = 2 * chips
    me, dev = _place(chips)
    t, d = z_ref.shape
    half = t // 2
    el, rows, fe = hid_ref.shape
    nch = d // cb
    deep = hring.shape[0]
    total = nch * el
    ff = w1_ref.shape[1]
    ng = ff // fb
    right, left, pair = dev(1, 0), dev(chips - 1, 0), dev(0, 1)

    def o_in(c, e, s):
        return [pltpu.make_async_copy(hid_ref.at[e], hring.at[s], osem.at[s, 0]),
                pltpu.make_async_copy(ue2_ref.at[e, :, pl.ds(c * cb, cb)], ering.at[s], osem.at[s, 1])]

    def f_in(g, s):
        col = pl.ds(pl.multiple_of(g * fb, fb), fb)
        return [pltpu.make_async_copy(w1_ref.at[:, col], fup.at[s, 0], fsem.at[s, 0]),
                pltpu.make_async_copy(w3_ref.at[:, col], fup.at[s, 1], fsem.at[s, 1]),
                pltpu.make_async_copy(w2_ref.at[col, :], fdn.at[s], fsem.at[s, 2])]

    for i in range(deep):
        for cp in o_in(0, i, i):
            cp.start()
    c_in = pltpu.make_async_copy(c_hbm, cbuf, csem)
    c_in.start()
    acc[...] = a_ref[...].astype(f32)
    _greet([right, left, pair])

    lo, hi = pl.ds(0, half), pl.ds(half, half)
    d2d = [_remote(p.at[1], got.at[c % 2], dsend.at[c], drecv.at[c], pair) for c in range(nch)]

    def hops(c):
        r = lambda i, src, dst, to: _remote(src, dst, rsend.at[c, i], rrecv.at[c, i], to)
        return (r(0, part.at[c, 1, lo], relay.at[c, 0], left), r(1, part.at[c, 1, hi], relay.at[c, 1], right),
                r(2, part.at[c, 0, hi], home.at[c, 0], left), r(3, part.at[c, 2, lo], home.at[c, 1], right),
                r(4, part.at[c, 0, lo], home.at[c, 2], left), r(5, part.at[c, 2, hi], home.at[c, 3], right))

    def chip_sums(c):
        d2d[c].wait()
        cs = slice(c * cb, (c + 1) * cb)
        for dx in (2, 1, 3):
            part[c, dx - 1] = p[0, dx] + got[c % 2, dx]
        acc[:, cs] += p[0, 0] + got[c % 2, 0]
        h = hops(c)
        for i in range(4):
            h[i].start()

    def relayed(c):
        h = hops(c)
        h[0].wait_recv()
        h[1].wait_recv()
        part[c, 0, lo] += relay[c, 0]
        part[c, 2, hi] += relay[c, 1]
        h[4].start()
        h[5].start()

    def arrived(c):
        h = hops(c)
        for i in range(2, 6):
            h[i].wait_recv()
        cs = slice(c * cb, (c + 1) * cb)
        acc[:half, cs] += home[c, 1] + home[c, 2]
        acc[half:, cs] += home[c, 0] + home[c, 3]

    for c in range(nch):
        def one(e, c=c):
            i = c * el + e
            s = lax.rem(i, deep)
            for cp in o_in(c, e, s):
                cp.wait()
            yy = _dot(hring[s], ering[s]).astype(bf16)
            for q in range(n):
                y[q, pl.ds(pl.multiple_of(e * cap, cap), cap), :] = yy[q * cap:(q + 1) * cap]

            @pl.when(e + deep < el)
            def _():
                for cp in o_in(c, e + deep, s):
                    cp.start()

            if c + 1 < nch:
                @pl.when(e + deep >= el)
                def _():
                    for cp in o_in(c + 1, e + deep - el, s):
                        cp.start()

        _loop(el, one)
        if c == 0:
            c_in.wait()
        if c >= 2:
            relayed(c - 2)
        if c >= 1:
            chip_sums(c - 1)

        def combine(q):
            r = _dot(cbuf[q], y[q])
            p[lax.rem(q, 2), q // 2] = r[:t] + r[t:2 * t] + r[2 * t:]

        _loop(n, combine)
        d2d[c].start()
        if c == 0:
            for s in range(2):
                for cp in f_in(s, s):
                    cp.start()

    events = {1: [lambda: relayed(nch - 2), lambda: chip_sums(nch - 1)], ng // 4: [lambda: arrived(0)],
              ng // 2: [lambda: arrived(1)], (5 * ng) // 8: [lambda: relayed(nch - 1)]}

    def group(g):
        s = lax.rem(g, 2)
        for cp in f_in(g, s):
            cp.wait()
        z = z_ref[...]
        h1 = _dot(z, fup[s, 0])
        h3 = _dot(z, fup[s, 1])
        acc[...] += _dot((h1 * jax.nn.sigmoid(h1) * h3).astype(bf16), fdn[s])

        @pl.when(g + 2 < ng)
        def _():
            for cp in f_in(g + 2, s):
                cp.start()

        for at, fs in events.items():
            @pl.when(g == at)
            def _(fs=fs):
                for f in fs:
                    f()

    _loop(ng, group)
    for c in range(2, nch):
        arrived(c)
    out_ref[...] = acc[...].astype(bf16)
    for c in range(nch):
        for h in hops(c):
            h.wait_send()


def _back(chips, cap, z, a, hid, c, ue2, w1, w3, w2, cb=512, fb=512, deep=4):
    t, d = z.shape
    el, rows, fe = hid.shape
    n = 2 * chips
    nch = d // cb
    vm, hbm = pl.BlockSpec(memory_space=pltpu.VMEM), pl.BlockSpec(memory_space=pl.ANY)
    dma = pltpu.SemaphoreType.DMA
    return pl.pallas_call(
        functools.partial(_back_kernel, chips, cap, cb, fb),
        in_specs=[vm] * 2 + [hbm] * 6,
        out_specs=vm,
        out_shape=jax.ShapeDtypeStruct((t, d), bf16),
        scratch_shapes=[
            pltpu.VMEM(c.shape, bf16), pltpu.VMEM((deep, rows, fe), bf16), pltpu.VMEM((deep, fe, cb), bf16),
            pltpu.VMEM((n, el * cap, cb), bf16), pltpu.VMEM((2, chips, t, cb), f32), pltpu.VMEM((2, chips, t, cb), f32),
            pltpu.VMEM((nch, 3, t, cb), f32), pltpu.VMEM((nch, 2, t // 2, cb), f32), pltpu.VMEM((nch, 4, t // 2, cb), f32),
            pltpu.VMEM((t, d), f32), pltpu.VMEM((2, 2, d, fb), bf16), pltpu.VMEM((2, fb, d), bf16),
            dma, dma((deep, 2)), dma((2, 3)), dma((nch,)), dma((nch,)), dma((nch, 6)), dma((nch, 6)),
        ],
        compiler_params=pltpu.CompilerParams(vmem_limit_bytes=63 * MiB, collective_id=1, has_side_effects=True),
        name="back",
    )(z, a, hid, c, ue2, w1, w3, w2)


def solution(mesh):
    G = mesh.shape['ep']

    def local(h0, idx, slot, na, wq, wk, wv, wo, nf, w1, w3, w2, nm, wr, ue1, ue3, ue2):
        b, s, d = h0.shape
        t = b * s
        k = idx.shape[-1]
        cap = 2 * t * k // (ue1.shape[0] * G)
        row = lambda w: w.reshape(1, d)
        ang = jnp.arange(s).astype(f32)[:, None] * (ROPE_BASE ** (-2.0 * jnp.arange(HEAD // 2).astype(f32) / HEAD))[None, :]
        cos, sin = jnp.cos(ang), jnp.sin(ang)
        hid, c, a, z = _front(G // 2, cap, h0.reshape(t, d), row(nm), wr.T, idx.reshape(t, k).T, slot.reshape(t, k).T,
                              row(na), row(nf), jnp.concatenate([cos, cos], 1), jnp.concatenate([-sin, sin], 1),
                              wq, wk, wv, wo, ue1, ue3)
        return _back(G // 2, cap, z, a, hid, c, ue2, w1, w3, w2).reshape(b, s, d)

    rows_spec = P(('dp', 'ep'))
    in_specs = (rows_spec,) * 3 + (P(),) * 11 + (P('ep'),) * 3
    return jax.shard_map(local, mesh=mesh, in_specs=in_specs, out_specs=rows_spec, check_vma=False)
```

time: 623 us -> 192 us (0.31); the launches traced: 613 us -> 192 us
  blocking collectives: 189 us -> 0 us
  Pallas kernels: 0 us -> 185 us
  matrix products: 144 us -> 0 us
  local copies, waits for them, and re-layouts: 146 us -> 6.18 us
  waiting for transfers between devices: 97.8 us -> 0 us
  other arithmetic: 27.7 us -> 1.39 us
  starting transfers between devices: 7.15 us -> 0 us
    all_to_all x1 -> x0, blocking collectives: 189 us -> none  [local(): recv = lax.all_to_all(send, 'ep', 0, 0, tiled=True)]
    pallas_call x0 -> x2, Pallas kernels: none -> 185 us  [the longest x1 96.2 us: _back(): pl.pallas_call(functools.partial(_back_kernel, chips, cap, cb, fb), in_sp...]
    dot_general x11 -> x0, matrix products: 144 us -> none  [the longest x1 45.4 us: _experts(): jnp.einsum('ecf,efd->ecd', hid, ue2, preferred_element_type=f32)]
    all_to_all x1 -> x0, waiting for transfers between devices: 97.8 us -> none  [local(): back = lax.all_to_all(y, 'ep', 0, 0, tiled=True)]
    gather x6 -> x0, local copies, waits for them, and re-layouts: 88.5 us -> none  [the longest x1 50.4 us: local(): yg = back[ix, sl]]
    dot_general x2 -> x0, local copies, waits for them, and re-layouts: 24.6 us -> none  [the longest x1 12.3 us: _dense(): jnp.dot(x, wk, preferred_element_type=f32).reshape(b, s, nkvv, HEAD)]
    transpose x2 -> x0, local copies, waits for them, and re-layouts: 20.7 us -> none  [the longest x1 14.1 us: local(): y = y.reshape(el, G, cap, d).transpose(1, 0, 2, 3).reshape(e, cap, d)]
    reduce_sum x4 -> x0, other arithmetic: 13.8 us -> none  [the longest x1 11.2 us: local(): m = jnp.sum(g[..., None] * yg.astype(f32), axis=1)]
  transfers between devices with their start and end apart: 1 -> 0, of which waited for: 1 -> 0; matrix products, arithmetic and copies ran while one was open for 14% -> 0% of each run, Pallas kernels for 0% -> 0%
where the time goes in v1:
time: 192 us
  Pallas kernels  185 us (96%)
  local copies, waits for them, and re-layouts  6.18 us (3%)
    pallas_call x1, Pallas kernels, _back(): pl.pallas_call(functools.partial(_back_kernel, chips, cap, cb, fb), in_sp...  96.2 us
    pallas_call x1, Pallas kernels, _front(): pl.pallas_call(functools.partial(_front_kernel, chips, k, cap, fb, hb), i...  88.3 us
    reshape x3, local copies, waits for them, and re-layouts, local(): row = lambda w: w.reshape(1, d)  3.87 us

profile of v1, /device:TPU:81, one launch (start us, length us, event | category | flops | bytes accessed | tf_op | source)
XLA Modules:
  0.0 192.1 jit_solution(206797807288607866)
XLA Ops:
  0.0 1.3 reshape.35.na_ref
  1.3 1.3 reshape.36.nf_ref
  2.6 1.3 reshape.32.nm_ref
  3.9 0.5 fusion
  4.4 0.8 pad_maximum_fusion
  5.3 88.3 %front.1 = (bf16[8,512,1024]{2,1,0:T(8,128)(2,1)}, bf16[8,768,512]{2,1,0:T(8,128)(2,1)}, bf16[256,2048]{1,0:T(8,128)(2,1)}, bf16[256,2048]{1,0:T(8,128)(2,1)}) custom-call(bf16[256,2048]{1,0:T(8,128)(2,1)} %bitcast.10, bf16[1,2048]{1,0:T(2,128)(2,1)} %reshape.32.nm_ref, bf16[64,2048]{1,0:T(8,128)(2,1)} %bitcast.11, s32[8,256]{1,0:T(8,128)} %bitcast.12, ...), custom_call_target="tpu_custom_call" | custom-call | tf_op jit(solution)/shard_map/front/pallas_call | solution.py:274
  93.6 96.2 %back.1 = bf16[256,2048]{1,0:T(8,128)(2,1)} custom-call(bf16[256,2048]{1,0:T(8,128)(2,1)} %get-tuple-element.9.z_ref, bf16[256,2048]{1,0:T(8,128)(2,1)} %get-tuple-element.10.a_ref, bf16[8,512,1024]{2,1,0:T(8,128)(2,1)} %get-tuple-element.11.hid_ref, bf16[8,768,512]{2,1,0:T(8,128)(2,1)} %get-tuple-element.12.c_hbm, bf16[8,1024,2048]{2,1,0:T(8,128)(2,1)} %ue2_ref.1, ...), custom_call_target="tpu_custom_call" | custom-call | tf_op jit(solution)/shard_map/back/pallas_call | solution.py:441
  189.8 2.3 %copy.19 = bf16[1,256,2048]{2,1,0:T(8,128)(2,1)} copy(bf16[1,256,2048]{2,1,0:T(8,128)(2,1)} %bitcast.9) | data formatting | bytes 2097152
  (2 shorter events, 0.0 us)

commit v2 on v1

v2 whole, which is shorter than its diff:
```python
import functools

import jax
import jax.numpy as jnp
import numpy as np
from jax import lax
from jax.experimental import pallas as pl
from jax.experimental.pallas import tpu as pltpu
from jax.sharding import PartitionSpec as P

HEAD = 128
EPS = 1e-6
ROPE_BASE = 10000.0
MiB = 1 << 20
f32, bf16 = jnp.float32, jnp.bfloat16
MESH = pl.DeviceIdType.MESH


def _dot(a, b):
    return jnp.dot(a, b, preferred_element_type=f32)


def _norm(x, w):
    xf = x.astype(f32)
    r = lax.rsqrt(jnp.mean(xf * xf, axis=-1, keepdims=True) + EPS)
    return (xf * r * w).astype(bf16)


def _row(w_ref):
    w = w_ref[...].astype(f32)
    return jnp.concatenate([w[i:i + 1, :] for i in range(w.shape[0])], axis=1)


def _loop(n, body):
    lax.fori_loop(0, n, lambda i, c: (body(i), c)[1], 0)


def _sources(chips):
    far = list(range(2, chips - 1))
    near = [1, chips - 1]
    return [(0, 0), (0, 1)] + [(x, c) for c in (0, 1) for x in near] + [(x, c) for x in far for c in (0, 1)]


def _place(chips):
    me = lax.axis_index('ep')
    x, c = me // 2, me % 2
    return me, lambda dx, fc: lax.rem(x + dx, chips) * 2 + (lax.rem(c + fc, 2))


def _remote(src, dst, ssem, rsem, dev):
    return pltpu.make_async_remote_copy(src_ref=src, dst_ref=dst, send_sem=ssem, recv_sem=rsem,
                                        device_id={'ep': dev}, device_id_type=MESH)


def _front_kernel(chips, k, cap, fb, hb,
                  h_ref, nm_ref, wrt_ref, idx_ref, slot_ref, na_ref, nf_ref, cos_ref, sin_ref,
                  wq_ref, wk_ref, wv_ref, wo_ref, ue1_ref, ue3_ref,
                  hid_ref, c_ref, a_ref, z_ref,
                  uall, maps, mall, xg, xa, acc, aring, bring, ering, hstage, cstage,
                  asem, esem, hsem, csem, usend, urecv, msend, mrecv):
    n = 2 * chips
    me, dev = _place(chips)
    t, d = h_ref.shape
    half = t // 2
    el = ue1_ref.shape[0]
    fe = ue1_ref.shape[2]
    wb = hb * HEAD
    ng = wq_ref.shape[1] // wb
    nf = fe // fb
    deep = ering.shape[0]

    def attn_in(g, s):
        col = pl.ds(pl.multiple_of(g * wb, wb), wb)
        return [pltpu.make_async_copy(w.at[:, col], aring.at[s, i], asem.at[s, i])
                for i, w in enumerate((wq_ref, wk_ref, wv_ref))] + [
            pltpu.make_async_copy(wo_ref.at[col, :], bring.at[s], asem.at[s, 3])]

    def exp_in(e, j, s):
        col = pl.ds(pl.multiple_of(j * fb, fb), fb)
        return [pltpu.make_async_copy(w.at[e, :, col], ering.at[s, q], esem.at[s, q])
                for q, w in enumerate((ue1_ref, ue3_ref))]

    for s in range(2):
        for cp in attn_in(s, s):
            cp.start()

    rel = _sources(chips)
    others = [dev(*r) for r in rel[1:]]
    bar = pltpu.get_barrier_semaphore()
    for o in others:
        pl.semaphore_signal(bar, inc=1, device_id={'ep': o}, device_id_type=MESH)
    u = _norm(h_ref[...], _row(nm_ref))
    uall[0] = u
    pl.semaphore_wait(bar, len(others))

    lo, hi, whole = pl.ds(0, half), pl.ds(half, half), pl.ds(0, t)
    right, left, pair = dev(1, 0), dev(chips - 1, 0), dev(0, 1)
    hop = lambda i, a, b, rows, to: _remote(uall.at[a, rows], uall.at[b, rows], usend.at[i], urecv.at[i], to)
    r1, l1 = hop(0, 0, 2, lo, right), hop(1, 0, 3, hi, left)
    r2, l2 = hop(2, 0, 2, hi, right), hop(3, 0, 3, lo, left)
    p0 = hop(4, 0, 1, whole, pair)
    ro, lo_ = hop(5, 2, 6, lo, right), hop(6, 3, 6, hi, left)
    p1, p3 = hop(7, 2, 4, whole, pair), hop(8, 3, 5, whole, pair)
    p2 = hop(9, 6, 7, whole, pair)
    for m in (r1, l1, p0):
        m.start()

    lt = lax.dot_general(wrt_ref[...], u, (((1,), (1,)), ((), ())), preferred_element_type=f32)
    ids = lax.broadcasted_iota(jnp.int32, lt.shape, 0)
    hits = [ids == idx_ref[j:j + 1, :] for j in range(k)]
    sel = [jnp.sum(jnp.where(h, lt, 0.0), axis=0, keepdims=True) for h in hits]
    top = functools.reduce(jnp.maximum, sel)
    ex = [jnp.exp(s - top) for s in sel]
    den = functools.reduce(jnp.add, ex)
    gate = jnp.zeros(lt.shape, f32)
    slot = jnp.full(lt.shape, -1.0, f32)
    for j in range(k):
        gate = jnp.where(hits[j], ex[j] / den, gate)
        slot = jnp.where(hits[j], slot_ref[j:j + 1, :].astype(f32), slot)
    maps[0] = slot
    maps[1] = gate
    xa[...] = _norm(h_ref[...], _row(na_ref))
    acc[...] = jnp.zeros_like(acc)

    own = pl.ds(pl.multiple_of(me * el, el), el)
    mall[0] = maps[:, own, :]

    metas = [_remote(maps.at[:, pl.ds(pl.multiple_of(o * el, el), el), :], mall.at[p + 1],
                     msend.at[p], mrecv.at[p], o) for p, o in enumerate(others)]
    for m in metas + [r2, l2]:
        m.start()
    for s in range(deep):
        for cp in exp_in(s // nf, s % nf, s):
            cp.start()

    def head_group(g):
        s = lax.rem(g, 2)
        for cp in attn_in(g, s):
            cp.wait()
        x = xa[...]
        q = _dot(x, aring[s, 0])
        kk = _dot(x, aring[s, 1])
        v = _dot(x, aring[s, 2]).astype(bf16)
        cos, sin = cos_ref[...], sin_ref[...]
        causal = lax.broadcasted_iota(jnp.int32, (t, t), 0) >= lax.broadcasted_iota(jnp.int32, (t, t), 1)
        outs = []
        for hd in range(hb):
            sl = slice(hd * HEAD, (hd + 1) * HEAD)
            qh = (q[:, sl] * cos + pltpu.roll(q[:, sl], HEAD // 2, 1) * sin).astype(bf16)
            kh = (kk[:, sl] * cos + pltpu.roll(kk[:, sl], HEAD // 2, 1) * sin).astype(bf16)
            sc = lax.dot_general(qh, kh, (((1,), (1,)), ((), ())), preferred_element_type=f32) * HEAD ** -0.5
            sc = jnp.where(causal, sc, -jnp.inf)
            e = jnp.exp(sc - jnp.max(sc, axis=-1, keepdims=True))
            pr = (e / jnp.sum(e, axis=-1, keepdims=True)).astype(bf16)
            outs.append(_dot(pr, v[:, sl]).astype(bf16))
        acc[...] += _dot(jnp.concatenate(outs, axis=1), bring[s])

        @pl.when(g + 2 < ng)
        def _():
            for cp in attn_in(g + 2, s):
                cp.start()

    _loop(ng, head_group)
    a = (h_ref[...].astype(f32) + acc[...]).astype(bf16)
    a_ref[...] = a
    z_ref[...] = _norm(a, _row(nf_ref))

    r1.wait_recv()
    l1.wait_recv()
    ro.start()
    lo_.start()

    for m in metas:
        m.wait_recv()
    tm = jnp.concatenate([mall[p, 0] for p in range(n)] + [mall[p, 1] for p in range(n)], axis=0).T
    g1 = tm.astype(bf16)
    r = tm - g1.astype(f32)
    g2 = r.astype(bf16)
    g3 = (r - g2.astype(f32)).astype(bf16)
    lanes = lax.broadcasted_iota(jnp.int32, (t, el * cap), 1)
    lane_slot = lax.rem(lanes, cap).astype(f32)
    rows_i = lax.broadcasted_iota(jnp.int32, (tm.shape[1], el * cap), 0)
    cols_e = lax.broadcasted_iota(jnp.int32, (tm.shape[1], el * cap), 1) // cap

    def c_out(s, b):
        return pltpu.make_async_copy(cstage.at[b], c_ref.at[s], csem.at[b])

    def gates(s):
        b = lax.rem(s, 2)

        @pl.when(s >= 2)
        def _():
            c_out(s - 2, b).wait()

        pick_s = (rows_i == cols_e + s * el).astype(f32).astype(bf16)
        pick_g = (rows_i == cols_e + (s + n) * el).astype(f32).astype(bf16)
        hit = _dot(g1, pick_s) == lane_slot
        for i, g in enumerate((g1, g2, g3)):
            cstage[b, i * t:(i + 1) * t, :] = jnp.where(hit, _dot(g, pick_g), 0.0).astype(bf16)
        c_out(s, b).start()

    _loop(n, gates)
    for s in range(n - 2, n):
        c_out(s, s % 2).wait()

    slots_i = lax.broadcasted_iota(jnp.int32, (cap, t), 0).astype(f32)
    hs = n // 2
    rows = hs * cap

    def h_out(e, b, part):
        return pltpu.make_async_copy(hstage.at[b], hid_ref.at[e, pl.ds(part * rows, rows)], hsem.at[b])

    def gather(part, first, last):
        def one(s):
            p = part * hs + s
            oh = jnp.concatenate([(slots_i == mall[p, 0, e:e + 1, :]).astype(f32).astype(bf16) for e in range(el)], axis=0)
            for c in range(0, d, 512):
                g = _dot(oh, uall[p, :, c:c + 512]).astype(bf16)
                for e in range(el):
                    xg[e, pl.ds(pl.multiple_of(s * cap, cap), cap), c:c + 512] = g[e * cap:(e + 1) * cap]
        lax.fori_loop(first, last, lambda i, c: (one(i), c)[1], 0)

    def hidden(part):
        def one(i):
            gi = part * el * nf + i
            e, j = i // nf, lax.rem(i, nf)
            b, s = lax.rem(e, 2), lax.rem(gi, deep)
            for cp in exp_in(e, j, s):
                cp.wait()
            x = xg[e]

            @pl.when((e >= 2) & (j == 0))
            def _():
                h_out(e - 2, b, part).wait()

            h1 = _dot(x, ering[s, 0])
            h3 = _dot(x, ering[s, 1])
            hstage[b, :, pl.ds(pl.multiple_of(j * fb, fb), fb)] = (h1 * jax.nn.sigmoid(h1) * h3).astype(bf16)

            @pl.when(j == nf - 1)
            def _():
                h_out(e, b, part).start()

            @pl.when(gi + deep < 2 * el * nf)
            def _():
                nx = lax.rem(i + deep, el * nf)
                for cp in exp_in(nx // nf, lax.rem(nx, nf), s):
                    cp.start()

            if part == 0:
                @pl.when(i == (3 * el * nf) // 4)
                def _():
                    ro.wait_recv()
                    lo_.wait_recv()
                    p2.start()
        _loop(el * nf, one)
        for e in range(el - 2, el):
            h_out(e, e % 2, part).wait()

    p0.wait_recv()
    gather(0, 0, 2)
    r2.wait_recv()
    l2.wait_recv()
    p1.start()
    p3.start()
    gather(0, 2, hs)
    hidden(0)
    p1.wait_recv()
    p3.wait_recv()
    p2.wait_recv()
    gather(1, 0, hs)
    hidden(1)
    for m in metas + [r1, l1, r2, l2, p0, ro, lo_, p1, p3, p2]:
        m.wait_send()


def _front(chips, cap, h, nm, wrt, idxt, slott, na, nf, cos, sin, wq, wk, wv, wo, ue1, ue3, fb=512, hb=4, deep=4):
    t, d = h.shape
    el, _, fe = ue1.shape
    n = 2 * chips
    k = idxt.shape[0]
    e = wrt.shape[0]
    vm, hbm = pl.BlockSpec(memory_space=pltpu.VMEM), pl.BlockSpec(memory_space=pl.ANY)
    dma = pltpu.SemaphoreType.DMA
    return pl.pallas_call(
        functools.partial(_front_kernel, chips, k, cap, fb, hb),
        in_specs=[vm] * 9 + [hbm] * 6,
        out_specs=[hbm, hbm, vm, vm],
        out_shape=(jax.ShapeDtypeStruct((el, n * cap, fe), bf16), jax.ShapeDtypeStruct((n, 3 * t, el * cap), bf16),
                   jax.ShapeDtypeStruct((t, d), bf16), jax.ShapeDtypeStruct((t, d), bf16)),
        scratch_shapes=[
            pltpu.VMEM((n, t, d), bf16), pltpu.VMEM((2, e, t), f32), pltpu.VMEM((n, 2, el, t), f32),
            pltpu.VMEM((el, n // 2 * cap, d), bf16), pltpu.VMEM((t, d), bf16), pltpu.VMEM((t, d), f32),
            pltpu.VMEM((2, 3, d, hb * HEAD), bf16), pltpu.VMEM((2, hb * HEAD, d), bf16),
            pltpu.VMEM((deep, 2, d, fb), bf16), pltpu.VMEM((2, n // 2 * cap, fe), bf16),
            pltpu.VMEM((2, 3 * t, el * cap), bf16),
            dma((2, 4)), dma((deep, 2)), dma((2,)), dma((2,)), dma((10,)), dma((10,)), dma((n - 1,)), dma((n - 1,)),
        ],
        compiler_params=pltpu.CompilerParams(vmem_limit_bytes=63 * MiB, collective_id=0, has_side_effects=True),
        name="front",
    )(h, nm, wrt, idxt, slott, na, nf, cos, sin, wq, wk, wv, wo, ue1, ue3)


def _back_kernel(chips, cap, cuts, fb, z_ref, a_ref, hid_ref, c_hbm, ue2_ref, w1_ref, w3_ref, w2_ref, out_ref,
                 cbuf, hbuf, ering, y, p, got, part, relay, home, acc, fup, fdn,
                 csem, hsem, osem, fsem, dsend, drecv, rsend, rrecv):
    n = 2 * chips
    rel = _sources(chips)
    me, dev = _place(chips)
    t, d = z_ref.shape
    half = t // 2
    el, rows, fe = hid_ref.shape
    nch = len(cuts) - 1
    cols = [pl.ds(cuts[c], cuts[c + 1] - cuts[c]) for c in range(nch)]
    wide = [pl.ds(0, cuts[c + 1] - cuts[c]) for c in range(nch)]
    deep = ering.shape[0]
    ff = w1_ref.shape[1]
    ng = ff // fb
    right, left, pair = dev(1, 0), dev(chips - 1, 0), dev(0, 1)

    def o_in(c, e, s):
        return pltpu.make_async_copy(ue2_ref.at[e, :, cols[c]], ering.at[s, :, wide[c]], osem.at[s])

    def h_in(e):
        return pltpu.make_async_copy(hid_ref.at[e], hbuf.at[e], hsem.at[e])

    def f_in(g, s):
        col = pl.ds(pl.multiple_of(g * fb, fb), fb)
        return [pltpu.make_async_copy(w1_ref.at[:, col], fup.at[s, 0], fsem.at[s, 0]),
                pltpu.make_async_copy(w3_ref.at[:, col], fup.at[s, 1], fsem.at[s, 1]),
                pltpu.make_async_copy(w2_ref.at[col, :], fdn.at[s], fsem.at[s, 2])]

    for i in range(el):
        h_in(i).start()
        if i < deep:
            o_in(0, i, i).start()
    c_in = pltpu.make_async_copy(c_hbm, cbuf, csem)
    c_in.start()
    bar = pltpu.get_barrier_semaphore()
    for o in (right, left, pair):
        pl.semaphore_signal(bar, inc=1, device_id={'ep': o}, device_id_type=MESH)
    acc[...] = a_ref[...].astype(f32)
    pl.semaphore_wait(bar, 3)

    lo, hi = pl.ds(0, half), pl.ds(half, half)
    d2d = [_remote(p.at[1, :, :, wide[c]], got.at[c % 2, :, :, wide[c]], dsend.at[c], drecv.at[c], pair)
           for c in range(nch)]

    def hops(c):
        w = cols[c]
        r = lambda i, src, dst, to: _remote(src, dst, rsend.at[c, i], rrecv.at[c, i], to)
        return (r(0, part.at[1, lo, w], relay.at[0, :, w], left), r(1, part.at[1, hi, w], relay.at[1, :, w], right),
                r(2, part.at[0, hi, w], home.at[0, :, w], left), r(3, part.at[2, lo, w], home.at[1, :, w], right),
                r(4, part.at[0, lo, w], home.at[2, :, w], left), r(5, part.at[2, hi, w], home.at[3, :, w], right))

    def chip_sums(c):
        d2d[c].wait()
        w, v = cols[c], wide[c]
        for dx in (2, 1, 3):
            part[dx - 1, :, w] = p[0, dx, :, v] + got[c % 2, dx, :, v]
        acc[:, w] += p[0, 0, :, v] + got[c % 2, 0, :, v]
        for h in hops(c)[:4]:
            h.start()

    def relayed(c):
        h = hops(c)
        w = cols[c]
        h[0].wait_recv()
        h[1].wait_recv()
        part[0, lo, w] += relay[0, :, w]
        part[2, hi, w] += relay[1, :, w]
        h[4].start()
        h[5].start()

    def arrived(c):
        for h in hops(c)[2:]:
            h.wait_recv()
        w = cols[c]
        acc[lo, w] += home[1, :, w] + home[2, :, w]
        acc[hi, w] += home[0, :, w] + home[3, :, w]

    for c in range(nch):
        v = wide[c]

        def two(i, c=c, v=v):
            es = [2 * i, 2 * i + 1]
            ring = [lax.rem(c * el + e, deep) for e in es]
            for e, s in zip(es, ring):
                o_in(c, e, s).wait()
                if c == 0:
                    h_in(e).wait()
            for e, s in zip(es, ring):
                yy = _dot(hbuf[e], ering[s, :, v]).astype(bf16)
                for q in range(n):
                    y[q, pl.ds(pl.multiple_of(e * cap, cap), cap), v] = yy[q * cap:(q + 1) * cap]

            @pl.when(2 * i + deep < el)
            def _():
                for e, s in zip(es, ring):
                    o_in(c, e + deep, s).start()

            if c + 1 < nch:
                @pl.when(2 * i + deep >= el)
                def _():
                    for e, s in zip(es, ring):
                        o_in(c + 1, e + deep - el, s).start()

        _loop(el // 2, two)
        if c == 0:
            c_in.wait()
        if c >= 1:
            chip_sums(c - 1)
        for q in range(n):
            yq = y[q, :, v]
            dx, fc = rel[q]
            p[fc, dx, :, v] = _dot(cbuf[q, :t], yq) + _dot(cbuf[q, t:2 * t], yq) + _dot(cbuf[q, 2 * t:], yq)
        d2d[c].start()
        if c == 0:
            for s in range(2):
                for cp in f_in(s, s):
                    cp.start()
        if c == 1:
            relayed(0)

    events = {0: [functools.partial(chip_sums, nch - 1)]}
    for c, g in zip(range(1, nch), (0, 1, 3, 6)):
        events.setdefault((ng * g) // 16, []).append(functools.partial(relayed, c))
    soon = nch // 2
    for c in range(soon):
        events.setdefault((ng * (3 + 5 * c)) // 16, []).append(functools.partial(arrived, c))

    def group(g):
        s = lax.rem(g, 2)
        for cp in f_in(g, s):
            cp.wait()
        z = z_ref[...]
        h1 = _dot(z, fup[s, 0])
        h3 = _dot(z, fup[s, 1])
        acc[...] += _dot((h1 * jax.nn.sigmoid(h1) * h3).astype(bf16), fdn[s])

        @pl.when(g + 2 < ng)
        def _():
            for cp in f_in(g + 2, s):
                cp.start()

        for at, fs in events.items():
            @pl.when(g == at)
            def _(fs=fs):
                for f in fs:
                    f()

    _loop(ng, group)
    for c in range(soon, nch):
        arrived(c)
    out_ref[...] = acc[...].astype(out_ref.dtype)
    for c in range(nch):
        for h in hops(c):
            h.wait_send()


def _back(chips, cap, z, a, hid, c, ue2, w1, w3, w2, cb=512, first=256, fb=512, deep=4):
    t, d = z.shape
    el, rows, fe = hid.shape
    n = 2 * chips
    cuts = (0,) + tuple(range(first, d, cb)) + (d,)
    nch = len(cuts) - 1
    vm, hbm = pl.BlockSpec(memory_space=pltpu.VMEM), pl.BlockSpec(memory_space=pl.ANY)
    dma = pltpu.SemaphoreType.DMA
    return pl.pallas_call(
        functools.partial(_back_kernel, chips, cap, cuts, fb),
        in_specs=[vm] * 2 + [hbm] * 6,
        out_specs=vm,
        out_shape=jax.ShapeDtypeStruct((t, d), bf16),
        scratch_shapes=[
            pltpu.VMEM(c.shape, bf16), pltpu.VMEM(hid.shape, bf16), pltpu.VMEM((deep, fe, cb), bf16),
            pltpu.VMEM((n, el * cap, cb), bf16), pltpu.VMEM((2, chips, t, cb), f32), pltpu.VMEM((2, chips, t, cb), f32),
            pltpu.VMEM((3, t, d), f32), pltpu.VMEM((2, t // 2, d), f32), pltpu.VMEM((4, t // 2, d), f32),
            pltpu.VMEM((t, d), f32), pltpu.VMEM((2, 2, d, fb), bf16), pltpu.VMEM((2, fb, d), bf16),
            dma, dma((el,)), dma((deep,)), dma((2, 3)), dma((nch,)), dma((nch,)), dma((nch, 6)), dma((nch, 6)),
        ],
        compiler_params=pltpu.CompilerParams(vmem_limit_bytes=63 * MiB, collective_id=1, has_side_effects=True),
        name="back",
    )(z, a, hid, c, ue2, w1, w3, w2)


def solution(mesh):
    G = mesh.shape['ep']

    def local(h0, idx, slot, na, wq, wk, wv, wo, nf, w1, w3, w2, nm, wr, ue1, ue3, ue2):
        b, s, d = h0.shape
        t = b * s
        k = idx.shape[-1]
        cap = 2 * t * k // (ue1.shape[0] * G)
        row = lambda w: w.reshape(d // HEAD, HEAD)
        inv = np.float32(ROPE_BASE) ** (np.arange(HEAD // 2).astype(np.float32) * np.float32(-2.0 / HEAD))
        ang = np.arange(s).astype(np.float32)[:, None] * inv[None, :]
        cos, sin = np.cos(ang), np.sin(ang)
        hid, c, a, z = _front(G // 2, cap, h0.reshape(t, d), row(nm), wr.T, idx.reshape(t, k).T, slot.reshape(t, k).T,
                              row(na), row(nf), np.concatenate([cos, cos], 1), np.concatenate([-sin, sin], 1),
                              wq, wk, wv, wo, ue1, ue3)
        return _back(G // 2, cap, z, a, hid, c, ue2, w1, w3, w2).reshape(b, s, d)

    rows_spec = P(('dp', 'ep'))
    in_specs = (rows_spec,) * 3 + (P(),) * 11 + (P('ep'),) * 3
    return jax.shard_map(local, mesh=mesh, in_specs=in_specs, out_specs=rows_spec, check_vma=False)
```

time: 192 us -> 176 us (0.917)
  Pallas kernels: 185 us -> 173 us
  local copies, waits for them, and re-layouts: 6.18 us -> 2.3 us
    pallas_call x1, Pallas kernels: 88.3 us -> 81.2 us  [_front(): pl.pallas_call(functools.partial(_front_kernel, chips, k, cap, fb, hb), i...]
    pallas_call x1, Pallas kernels: 96.2 us -> 91.9 us  [_back(): pl.pallas_call(functools.partial(_back_kernel, chips, cap, cuts, fb), in_...]
    reshape x3 -> x0, local copies, waits for them, and re-layouts: 3.87 us -> none  [local(): row = lambda w: w.reshape(1, d)]
where the time goes in v2:
time: 176 us; the launch traced here: 175 us
  Pallas kernels  173 us (98%)
  local copies, waits for them, and re-layouts  2.3 us (1%)
    pallas_call x1, Pallas kernels, _back(): pl.pallas_call(functools.partial(_back_kernel, chips, cap, cuts, fb), in_...  91.9 us
    pallas_call x1, Pallas kernels, _front(): pl.pallas_call(functools.partial(_front_kernel, chips, k, cap, fb, hb), i...  81.2 us

profile of v2, /device:TPU:81, one launch (start us, length us, event | category | flops | bytes accessed | tf_op | source)
XLA Modules:
  0.0 175.5 jit_solution(11591160128867173162)
XLA Ops:
  0.0 81.2 %front.1 = (bf16[8,512,1024]{2,1,0:T(8,128)(2,1)}, bf16[8,768,512]{2,1,0:T(8,128)(2,1)}, bf16[256,2048]{1,0:T(8,128)(2,1)}, bf16[256,2048]{1,0:T(8,128)(2,1)}) custom-call(bf16[256,2048]{1,0:T(8,128)(2,1)} %bitcast.13, bf16[16,128]{1,0:T(8,128)(2,1)} %bitcast.17, bf16[64,2048]{1,0:T(8,128)(2,1)} %bitcast.14, s32[8,256]{1,0:T(8,128)} %bitcast.15, ...), custom_call_target="tpu_custom_call" | custom-call | tf_op jit(solution)/shard_map/front/pallas_call | solution.py:285
  81.2 91.9 %back.1 = bf16[256,2048]{1,0:T(8,128)(2,1)} custom-call(bf16[256,2048]{1,0:T(8,128)(2,1)} %get-tuple-element.9.z_ref, bf16[256,2048]{1,0:T(8,128)(2,1)} %get-tuple-element.10.a_ref, bf16[8,512,1024]{2,1,0:T(8,128)(2,1)} %get-tuple-element.11.hid_ref, bf16[8,768,512]{2,1,0:T(8,128)(2,1)} %get-tuple-element.12.c_hbm, bf16[8,1024,2048]{2,1,0:T(8,128)(2,1)} %ue2_ref.1, ...), custom_call_target="tpu_custom_call" | custom-call | tf_op jit(solution)/shard_map/back/pallas_call | solution.py:469
  173.2 2.3 %copy.21 = bf16[1,256,2048]{2,1,0:T(8,128)(2,1)} copy(bf16[1,256,2048]{2,1,0:T(8,128)(2,1)} %bitcast.12) | data formatting | bytes 2097152

commit v3 on v2

--- a/solution.py
+++ b/solution.py
@@ -76,7 +76,7 @@
             pltpu.make_async_copy(wo_ref.at[col, :], bring.at[s], asem.at[s, 3])]
 
     def exp_in(e, j, s):
-        col = pl.ds(pl.multiple_of(j * fb, fb), fb)
+        col = pl.ds(j * fb, fb)
         return [pltpu.make_async_copy(w.at[e, :, col], ering.at[s, q], esem.at[s, q])
                 for q, w in enumerate((ue1_ref, ue3_ref))]
 
@@ -151,7 +151,7 @@
             sc = lax.dot_general(qh, kh, (((1,), (1,)), ((), ())), preferred_element_type=f32) * HEAD ** -0.5
             sc = jnp.where(causal, sc, -jnp.inf)
             e = jnp.exp(sc - jnp.max(sc, axis=-1, keepdims=True))
-            pr = (e / jnp.sum(e, axis=-1, keepdims=True)).astype(bf16)
+            pr = (e * (1.0 / jnp.sum(e, axis=-1, keepdims=True))).astype(bf16)
             outs.append(_dot(pr, v[:, sl]).astype(bf16))
         acc[...] += _dot(jnp.concatenate(outs, axis=1), bring[s])
 
@@ -221,39 +221,38 @@
         lax.fori_loop(first, last, lambda i, c: (one(i), c)[1], 0)
 
     def hidden(part):
-        def one(i):
-            gi = part * el * nf + i
-            e, j = i // nf, lax.rem(i, nf)
-            b, s = lax.rem(e, 2), lax.rem(gi, deep)
-            for cp in exp_in(e, j, s):
-                cp.wait()
-            x = xg[e]
-
-            @pl.when((e >= 2) & (j == 0))
+        def one(e, refill):
+            b = lax.rem(e, 2)
+            ring = [lax.rem((part * el + e) * nf + j, deep) for j in range(nf)]
+
+            @pl.when(e >= 2)
             def _():
                 h_out(e - 2, b, part).wait()
 
-            h1 = _dot(x, ering[s, 0])
-            h3 = _dot(x, ering[s, 1])
-            hstage[b, :, pl.ds(pl.multiple_of(j * fb, fb), fb)] = (h1 * jax.nn.sigmoid(h1) * h3).astype(bf16)
-
-            @pl.when(j == nf - 1)
-            def _():
-                h_out(e, b, part).start()
-
-            @pl.when(gi + deep < 2 * el * nf)
-            def _():
-                nx = lax.rem(i + deep, el * nf)
-                for cp in exp_in(nx // nf, lax.rem(nx, nf), s):
-                    cp.start()
-
             if part == 0:
-                @pl.when(i == (3 * el * nf) // 4)
+                @pl.when(e == (3 * el) // 4)
                 def _():
                     ro.wait_recv()
                     lo_.wait_recv()
                     p2.start()
-        _loop(el * nf, one)
+
+            for j in range(nf):
+                for cp in exp_in(e, j, ring[j]):
+                    cp.wait()
+            for j in range(nf):
+                for c in range(0, fb, 256):
+                    h1 = _dot(xg[e], ering[ring[j], 0, :, c:c + 256])
+                    h3 = _dot(xg[e], ering[ring[j], 1, :, c:c + 256])
+                    hstage[b, :, j * fb + c:j * fb + c + 256] = (h1 * jax.nn.sigmoid(h1) * h3).astype(bf16)
+                if refill:
+                    for cp in exp_in(lax.rem(e + deep // nf, el), j, ring[j]):
+                        cp.start()
+            h_out(e, b, part).start()
+
+        ahead = deep // nf if part == 1 else 0
+        lax.fori_loop(0, el - ahead, lambda e, c: (one(e, True), c)[1], 0)
+        if ahead:
+            lax.fori_loop(el - ahead, el, lambda e, c: (one(e, False), c)[1], 0)
         for e in range(el - 2, el):
             h_out(e, e % 2, part).wait()
 
@@ -379,6 +378,13 @@
         acc[lo, w] += home[1, :, w] + home[2, :, w]
         acc[hi, w] += home[0, :, w] + home[3, :, w]
 
+    sums, pass_on, home_in = chip_sums, relayed, arrived
+    after_y = {2: [(pass_on, 0), (sums, 1)], 3: [(sums, 2)], 4: [(sums, 3), (pass_on, 2)],
+               5: [(pass_on, 3), (sums, 4)]}
+    after_c = {3: [(pass_on, 1)]}
+    after_f = {2: [(sums, 5)], 3: [(pass_on, 4)], 4: [(home_in, 0)], 5: [(home_in, 1)], 6: [(home_in, 2)],
+               7: [(home_in, 3)], 9: [(pass_on, 5)]}
+
     for c in range(nch):
         v = wide[c]
 
@@ -394,6 +400,11 @@
                 for q in range(n):
                     y[q, pl.ds(pl.multiple_of(e * cap, cap), cap), v] = yy[q * cap:(q + 1) * cap]
 
+            if c == 1:
+                @pl.when(i == el // 4)
+                def _():
+                    chip_sums(0)
+
             @pl.when(2 * i + deep < el)
             def _():
                 for e, s in zip(es, ring):
@@ -408,8 +419,8 @@
         _loop(el // 2, two)
         if c == 0:
             c_in.wait()
-        if c >= 1:
-            chip_sums(c - 1)
+        for f, i in after_y.get(c, ()):
+            f(i)
         for q in range(n):
             yq = y[q, :, v]
             dx, fc = rel[q]
@@ -419,15 +430,8 @@
             for s in range(2):
                 for cp in f_in(s, s):
                     cp.start()
-        if c == 1:
-            relayed(0)
-
-    events = {0: [functools.partial(chip_sums, nch - 1)]}
-    for c, g in zip(range(1, nch), (0, 1, 3, 6)):
-        events.setdefault((ng * g) // 16, []).append(functools.partial(relayed, c))
-    soon = nch // 2
-    for c in range(soon):
-        events.setdefault((ng * (3 + 5 * c)) // 16, []).append(functools.partial(arrived, c))
+        for f, i in after_c.get(c, ()):
+            f(i)
 
     def group(g):
         s = lax.rem(g, 2)
@@ -443,14 +447,14 @@
             for cp in f_in(g + 2, s):
                 cp.start()
 
-        for at, fs in events.items():
-            @pl.when(g == at)
+        for at, fs in after_f.items():
+            @pl.when(g == (at * ng) // 16)
             def _(fs=fs):
-                for f in fs:
-                    f()
+                for f, i in fs:
+                    f(i)
 
     _loop(ng, group)
-    for c in range(soon, nch):
+    for c in range(4, nch):
         arrived(c)
     out_ref[...] = acc[...].astype(out_ref.dtype)
     for c in range(nch):
@@ -458,11 +462,11 @@
             h.wait_send()
 
 
-def _back(chips, cap, z, a, hid, c, ue2, w1, w3, w2, cb=512, first=256, fb=512, deep=4):
+def _back(chips, cap, z, a, hid, c, ue2, w1, w3, w2, cb=512, fb=512, deep=4):
     t, d = z.shape
     el, rows, fe = hid.shape
     n = 2 * chips
-    cuts = (0,) + tuple(range(first, d, cb)) + (d,)
+    cuts = tuple(i * d // 8 for i in (0, 1, 2, 3, 4, 6, 8))
     nch = len(cuts) - 1
     vm, hbm = pl.BlockSpec(memory_space=pltpu.VMEM), pl.BlockSpec(memory_space=pl.ANY)
     dma = pltpu.SemaphoreType.DMA

time: 176 us -> 171 us (0.972)
  Pallas kernels: 173 us -> 168 us
    pallas_call x1, Pallas kernels: 91.9 us -> 88.6 us  [_back(): pl.pallas_call(functools.partial(_back_kernel, chips, cap, cuts, fb), in_...]
    pallas_call x1, Pallas kernels: 81.2 us -> 79.1 us  [_front(): pl.pallas_call(functools.partial(_front_kernel, chips, k, cap, fb, hb), i...]
where the time goes in v3:
time: 171 us; the launch traced here: 170 us
  Pallas kernels  168 us (98%)
  local copies, waits for them, and re-layouts  2.3 us (1%)
    pallas_call x1, Pallas kernels, _back(): pl.pallas_call(functools.partial(_back_kernel, chips, cap, cuts, fb), in_...  88.6 us
    pallas_call x1, Pallas kernels, _front(): pl.pallas_call(functools.partial(_front_kernel, chips, k, cap, fb, hb), i...  79.1 us

profile of v3, /device:TPU:81, one launch (start us, length us, event | category | flops | bytes accessed | tf_op | source)
XLA Modules:
  0.0 170.1 jit_solution(9120403701420801272)
XLA Ops:
  0.0 79.1 %front.1 = (bf16[8,512,1024]{2,1,0:T(8,128)(2,1)}, bf16[8,768,512]{2,1,0:T(8,128)(2,1)}, bf16[256,2048]{1,0:T(8,128)(2,1)}, bf16[256,2048]{1,0:T(8,128)(2,1)}) custom-call(bf16[256,2048]{1,0:T(8,128)(2,1)} %bitcast.13, bf16[16,128]{1,0:T(8,128)(2,1)} %bitcast.17, bf16[64,2048]{1,0:T(8,128)(2,1)} %bitcast.14, s32[8,256]{1,0:T(8,128)} %bitcast.15, ...), custom_call_target="tpu_custom_call" | custom-call | tf_op jit(solution)/shard_map/front/pallas_call | solution.py:284
  79.1 88.6 %back.1 = bf16[256,2048]{1,0:T(8,128)(2,1)} custom-call(bf16[256,2048]{1,0:T(8,128)(2,1)} %get-tuple-element.9.z_ref, bf16[256,2048]{1,0:T(8,128)(2,1)} %get-tuple-element.10.a_ref, bf16[8,512,1024]{2,1,0:T(8,128)(2,1)} %get-tuple-element.11.hid_ref, bf16[8,768,512]{2,1,0:T(8,128)(2,1)} %get-tuple-element.12.c_hbm, bf16[8,1024,2048]{2,1,0:T(8,128)(2,1)} %ue2_ref.1, ...), custom_call_target="tpu_custom_call" | custom-call | tf_op jit(solution)/shard_map/back/pallas_call | solution.py:473
  167.8 2.3 %copy.21 = bf16[1,256,2048]{2,1,0:T(8,128)(2,1)} copy(bf16[1,256,2048]{2,1,0:T(8,128)(2,1)} %bitcast.12) | data formatting | bytes 2097152
